TPU v7x, 512 devices: a whole 4x8x8 slice. The times are simulated.
512 devices in a mesh: modes: 16 (over y, core), gz: 32 (over x, z).
Axes of the slice: x: 4, y: 8, z: 8, core: 2. Of those that a mesh axis runs over, the one named last changes fastest.
Arguments:
- source_field: float32 [512, 2, 32, 2048], P('gz', None, None, 'modes'), may hold values from -0.075 to 0.075
- coupling_below: float32 [512], P('gz'), may hold values from 0.5 to 2
- coupling_above: float32 [512], P('gz'), may hold values from 0.5 to 2
- eigen_stream: float32 [32], replicated, may hold values from 0.000390625 to 0.015625
- eigen_span: float32 [2048], replicated, may hold values from 0.000390625 to 0.015625
Outputs:
- pressure: float32 [512, 2, 32, 2048], P('gz', None, 'modes')
All inputs are finite; a program needn't handle non-finite values.
Results may differ from a plain program's by a relative error of at most 0.0003.
Values sent between devices are 32-bit elements; how exact they have to be, the bound alone decides.
A program may use at most 64 MiB of HBM per device.

v0:
```python
import jax
import jax.numpy as jnp
from jax import lax
from jax.sharding import PartitionSpec as P


def shifted(array, axis, by):
    count = lax.axis_size(axis)
    pairs = [(i, i + by) for i in range(count) if 0 <= i + by < count]
    return lax.ppermute(array, axis, pairs)


def thomas(lower_row, upper_row, spectral, sources, initial):
    row_count = sources.shape[0]

    def thomas_forward(carried, inputs):
        factor, partial_value = carried
        lower_val, upper_val, source_row = inputs
        pivots = lower_val + upper_val + spectral - lower_val * factor
        partial_value = (source_row + lower_val * partial_value) / pivots
        factor = upper_val / pivots
        return ((factor, partial_value), (factor, partial_value))

    _, (factors, partials) = lax.scan(
        thomas_forward,
        (jnp.zeros_like(spectral), initial),
        (lower_row, upper_row, sources),
        unroll=True,
    )
    retain = (jnp.arange(row_count) < row_count - 1).astype(jnp.float32)
    factors = factors * retain.reshape((row_count,) + (1,) * spectral.ndim)

    def thomas_backward(behind, inputs):
        factor, partial_value = inputs
        result = partial_value + factor * behind
        return (result, result)

    _, solved = lax.scan(
        thomas_backward, jnp.zeros_like(initial), (factors, partials), reverse=True, unroll=True
    )
    return solved


def reduced_solve(coeffs, right_side):

    def reduced_forward(carried, inputs):
        factor, partial_value = carried
        coeff_row, right_row = inputs
        pivots = coeff_row[1] - coeff_row[0] * factor
        factor = coeff_row[2] / pivots
        partial_value = (right_row - coeff_row[0] * partial_value) / pivots
        return ((factor, partial_value), (factor, partial_value))

    initial = (jnp.zeros_like(coeffs[0, 0]), jnp.zeros_like(right_side[0]))
    _, (factors, partials) = lax.scan(reduced_forward, initial, (coeffs, right_side), unroll=True)

    def reduced_backward(behind, inputs):
        factor, partial_value = inputs
        result = partial_value - factor * behind
        return (result, result)

    _, values = lax.scan(
        reduced_backward,
        jnp.zeros_like(right_side[0]),
        (factors, partials),
        reverse=True,
        unroll=True,
    )
    return values


def interfaces(planes, lower_row, upper_row, spectral):
    row_count = planes.shape[0]
    interior = row_count - 1
    modes_flat = planes.shape[2]
    last_mask = (jnp.arange(interior) == interior - 1).astype(jnp.float32) * upper_row[:interior]
    extra_source = last_mask[:, None, None] * jnp.ones((1, 1, modes_flat), jnp.float32)
    sources = jnp.concatenate(
        [planes[:interior], jnp.zeros((interior, 1, modes_flat), jnp.float32), extra_source], axis=1
    )
    initial = jnp.zeros((4, modes_flat), jnp.float32).at[2].set(1.0)
    solved = thomas(lower_row[:interior], upper_row[:interior], spectral, sources, initial)
    from_above = shifted(solved[0], "gz", -1)
    last_row = solved[interior - 1]
    lower_last = lower_row[row_count - 1]
    upper_last = upper_row[row_count - 1]
    coupling_down = -lower_last * last_row[2]
    central = (
        lower_last + upper_last + spectral - lower_last * last_row[3] - upper_last * from_above[2]
    )
    coupling_up = -upper_last * from_above[3]
    right_side = planes[row_count - 1] + lower_last * last_row[:2] + upper_last * from_above[:2]
    coeffs = jnp.stack([coupling_down, central, coupling_up])
    return (solved, coeffs, right_side)


def assemble(solved, interface_values):
    own_value = interface_values[:2]
    prev_value = interface_values[2:]
    inner = solved[:, :2] + solved[:, 2:3] * prev_value[None] + solved[:, 3:4] * own_value[None]
    return jnp.concatenate([inner, own_value[None]], axis=0)


def per_device(source_field, coupling_below, coupling_above, eigen_stream, eigen_span):
    arrived = lax.all_to_all(source_field, "modes", split_axis=2, concat_axis=3, tiled=True)
    row_count, _, kx_count, ky_count = arrived.shape
    partitions = lax.axis_size("gz")
    gz_index = lax.axis_index("gz")
    offset = lax.axis_index("modes") * kx_count
    stream_part = lax.dynamic_slice_in_dim(eigen_stream, offset, kx_count)
    spectral = stream_part[:, None] + eigen_span[None, :]
    global_row = gz_index * row_count + jnp.arange(row_count)
    lower_row = jnp.where(global_row == 0, 0.0, coupling_below)
    upper_row = jnp.where(global_row == row_count * partitions - 1, 0.0, coupling_above)
    modes_flat = kx_count * ky_count
    planes = arrived.reshape(row_count, 2, modes_flat)
    solved, coeffs, right_side = interfaces(planes, lower_row, upper_row, spectral.reshape(-1))
    coeff_items = coeffs.reshape(1, 3, kx_count, ky_count)
    right_items = right_side.reshape(1, 2, kx_count, ky_count)
    values = reduced_solve(
        lax.all_to_all(coeff_items, "gz", split_axis=3, concat_axis=0, tiled=True),
        lax.all_to_all(right_items, "gz", split_axis=3, concat_axis=0, tiled=True),
    )
    below_values = jnp.concatenate([jnp.zeros_like(values[:1]), values[:-1]], axis=0)
    paired = jnp.concatenate([values, below_values], axis=1)
    interface_values = lax.all_to_all(paired, "gz", split_axis=0, concat_axis=3, tiled=True)
    pressure = assemble(solved, interface_values.reshape(4, modes_flat))
    return pressure.reshape(row_count, 2, kx_count, ky_count)


def solution(mesh):
    in_specs = (P("gz", None, None, "modes"), P("gz"), P("gz"), P(), P())
    out_specs = P("gz", None, "modes", None)
    return jax.shard_map(
        per_device, mesh=mesh, in_specs=in_specs, out_specs=out_specs, check_vma=False
    )
```

profile of v0, /device:TPU:1, one launch (start us, length us, event | category | flops | bytes accessed | tf_op | source)
XLA Modules:
  0.0 165.4 jit_solution(2649458784567353007)
XLA Ops:
  0.0 2.2 %copy.185 = f32[16,2,32,128]{3,0,1,2:T(8,128)} copy(f32[16,2,32,128]{3,2,1,0:T(8,128)} %param.7) | data formatting | bytes 1048576 | tf_op args[0]
  2.2 10.2 %all-to-all-start = ((f32[16,2,32,128]{3,0,1,2:T(8,128)}), f32[16,2,32,128]{3,0,1,2:T(8,128)S(1)}, u32[]{:S(2)}, u32[]{:S(2)}) async-start(f32[16,2,32,128]{3,0,1,2:T(8,128)} %copy.185), calls=%async_computation | async-start | bytes 1048576 | tf_op jit(solution)/shard_map/all_to_all | solution.py:105
  12.4 0.7 fusion.65
  13.2 0.7 fusion.66
  15.8 0.6 divide_bitcast_fusion
  35.2 0.3 fusion.49
  36.1 17.8 %subtract_divide_fusion = (f32[1,4096]{1,0:T(1,128)S(1)}, f32[1,4096]{1,0:T(1,128)S(1)}, f32[1,4096]{1,0:T(1,128)S(1)}, f32[1,4096]{1,0:T(1,128)S(1)}, f32[1,409...) fusion(f32[1,4096]{1,0:T(1,128)S(1)} %bitcast.591, ...), kind=kLoop, calls=%fused_computation.222 | loop fusion | flops 172032 | bytes 475248 | tf_op jit(solution)/shard_map/eval_jaxpr/div | solution.py:21
  53.9 0.4 concatenate.33
  54.4 17.6 %multiply_subtract_fusion = (f32[4096]{0:T(1024)S(1)}, f32[4096]{0:T(1024)S(1)}, f32[4096]{0:T(1024)S(1)}, f32[4096]{0:T(1024)S(1)}, f32[4096]{0:T(1024)S(1)}, /...) fusion(f32[4096]{0:T(1024)S(1)} %bitcast.590, ...), kind=kLoop, calls=%fused_computation.208 | loop fusion | flops 172032 | bytes 475248 | tf_op jit(solution)/shard_map/eval_jaxpr/sub | solution.py:19
  73.4 0.2 slice_multiply_fusion.6
  73.6 0.3 copy.294
  74.0 0.3 slice.987
  74.2 0.2 mul.11727
  74.4 0.5 pad_maximum_fusion
  74.9 9.9 %multiply_add_fusion = (f32[4,4096]{1,0:T(4,128)S(1)}, f32[4,4096]{1,0:T(4,128)S(1)}) fusion(f32[4096]{0:T(1024)S(1)} %bitcast.556, f32[4096]{0:T(1024)S(1)} %bitcast.561, f32[4096]{0:T(1024)S(1)} %bitcast.538, f32[4096]{0:T(1024)S(1)} %bitcast.563, f32[4096]{0:T(1024)S(1)} %bitcast.541, f32[4096]{0:T(1024)S(1)} %bitcast.565, f32[4096]{0:T(1024)S(1)} %bitcast.544, ...), kind=kLoop, calls=%fused_computation.134 | loop fusion | flops 1212416 | bytes 1671228 | tf_op jit(solution)/shard_map/eval_jaxpr/add | solution.py:35
  84.8 1.3 collective-permute-start
  86.1 9.9 %constant_dynamic-update-slice_fusion.14 = (f32[15,4,4096]{2,1,0:T(4,128)S(1)}, f32[1,4,4096]{2,1,0:T(4,128)S(1)}, f32[1,4,4096]{2,1,0:T(4,128)S(1)}, f32[1,4,40...) fusion(f32[4096]{0:T(1024)S(1)} %bitcast.574, ...), kind=kLoop, calls=%fused_computation.22 | loop fusion | flops 1212415 | bytes 2457660
  96.3 0.7 constant_dynamic-update-slice_fusion.1
  97.0 0.7 constant_dynamic-update-slice_fusion
  97.7 1.4 fusion.53
  99.2 1.3 fusion.18
  100.6 1.1 copy.187
  101.7 3.5 %reshape.17010 = f32[32,1,256]{2,1,0:T(1,128)} reshape(f32[2048,1,2,2]{3,2,1,0:T(2,128)S(1)} %bitcast.515) | data formatting | bytes 65536
  105.2 12.2 %all-to-all-start.1 = ((f32[32,1,256]{2,1,0:T(1,128)}), f32[32,1,256]{2,1,0:T(1,128)S(1)}, u32[]{:S(2)}, u32[]{:S(2)}) async-start(f32[32,1,256]{2,1,0:T(1,128)} %reshape.17010), calls=%async_computation.1 | async-start | bytes 65536 | tf_op jit(solution)/shard_map/all_to_all | solution.py:122
  117.4 1.1 copy.190
  118.5 3.6 %reshape.17012 = f32[32,1,384]{2,1,0:T(1,128)} reshape(f32[2048,1,2,3]{3,2,1,0:T(2,128)S(1)} %bitcast.516) | data formatting | bytes 98304
  122.1 4.0 %all-to-all-done.1 = f32[32,1,256]{2,1,0:T(1,128)S(1)} async-done(((f32[32,1,256]{2,1,0:T(1,128)}), f32[32,1,256]{2,1,0:T(1,128)S(1)}, u32[]{:S(2)}, u32[]{:S(2)}) %all-to-all-start.1) | async-done | bytes 32800 | tf_op jit(solution)/shard_map/all_to_all | solution.py:122
  126.2 5.2 %all-to-all-start.2 = ((f32[32,1,384]{2,1,0:T(1,128)}), f32[32,1,384]{2,1,0:T(1,128)S(1)}, u32[]{:S(2)}, u32[]{:S(2)}) async-start(f32[32,1,384]{2,1,0:T(1,128)} %reshape.17012), calls=%async_computation.2 | async-start | bytes 98304 | tf_op jit(solution)/shard_map/all_to_all | solution.py:121
  131.4 0.5 broadcast.15420
  131.9 0.7 reduce.15
  132.6 3.2 %reshape.17011 = f32[2048,1,2,2]{3,2,1,0:T(2,128)S(1)} reshape(f32[32,256]{1,0:T(8,128)S(1)} %reduce.15) | data formatting | bytes 65536
  135.8 1.0 copy.225
  136.9 3.3 %all-to-all-done.2 = f32[32,1,384]{2,1,0:T(1,128)S(1)} async-done(((f32[32,1,384]{2,1,0:T(1,128)}), f32[32,1,384]{2,1,0:T(1,128)S(1)}, u32[]{:S(2)}, u32[]{:S(2)}) %all-to-all-start.2) | async-done | bytes 49184 | tf_op jit(solution)/shard_map/all_to_all | solution.py:121
  140.2 0.7 reduce.14
  141.0 3.1 %reshape.17013 = f32[2048,1,2,3]{3,2,1,0:T(2,128)S(1)} reshape(f32[32,384]{1,0:T(8,128)S(1)} %reduce.14) | data formatting | bytes 98304
  144.1 1.0 copy.226
  145.3 0.4 divide_multiply_fusion
  145.6 0.2 subtract_divide_fusion.14
  146.4 0.8 reshape.17014
  147.2 6.0 %all-to-all-start.3 = ((f32[32,1,512]{2,1,0:T(1,128)}), f32[32,1,512]{2,1,0:T(1,128)S(1)}, u32[]{:S(2)}, u32[]{:S(2)}) async-start(f32[32,1,512]{2,1,0:T(1,128)} %reshape.17014), calls=%async_computation.3 | async-start | bytes 131072 | tf_op jit(solution)/shard_map/all_to_all | solution.py:126
  153.2 0.5 fusion.57
  153.7 0.1 copy.296
  153.9 0.1 copy.295
  154.0 8.0 %all-to-all-done.3 = f32[32,1,512]{2,1,0:T(1,128)S(1)} async-done(((f32[32,1,512]{2,1,0:T(1,128)}), f32[32,1,512]{2,1,0:T(1,128)S(1)}, u32[]{:S(2)}, u32[]{:S(2)}) %all-to-all-start.3) | async-done | bytes 65568 | tf_op jit(solution)/shard_map/all_to_all | solution.py:126
  162.0 0.8 reduce.16
  163.3 0.4 fusion
  163.7 0.6 concatenate.39
  164.3 1.1 pad_maximum_fusion.1
  (120 shorter events, 2.2 us)
Async XLA Ops:
  0.0 12.4 %copy-start.4 = (f32[16]{0:T(128)S(1)}, f32[16]{0:T(128)}, u32[]{:S(2)}) copy-start(f32[16]{0:T(128)} %param.9) | copy-start | bytes 196
  0.0 12.4 %copy-start.3 = (f32[16]{0:T(128)S(1)}, f32[16]{0:T(128)}, u32[]{:S(2)}) copy-start(f32[16]{0:T(128)} %param.8) | copy-start | bytes 196
  0.0 15.7 %copy-start.5 = (f32[32]{0:T(128)S(1)}, f32[32]{0:T(128)}, u32[]{:S(2)}) copy-start(f32[32]{0:T(128)} %param.10) | copy-start | bytes 388
  0.0 15.8 %copy-start.2 = (f32[2048]{0:T(1024)S(1)}, f32[2048]{0:T(1024)}, u32[]{:S(2)}) copy-start(f32[2048]{0:T(1024)} %param.11) | copy-start | bytes 24580
  2.2 71.4 %all-to-all-start = ((f32[16,2,32,128]{3,0,1,2:T(8,128)}), f32[16,2,32,128]{3,0,1,2:T(8,128)S(1)}, u32[]{:S(2)}, u32[]{:S(2)}) async-start(f32[16,2,32,128]{3,0,1,2:T(8,128)} %copy.185), calls=%async_computation | async-start | bytes 1048576 | tf_op jit(solution)/shard_map/all_to_all | solution.py:105
  73.9 1.0 copy-start.1
  74.2 11.9 %copy-start = (f32[1,4,4096]{2,1,0:T(4,128)S(1)}, f32[1,4,4096]{2,1,0:T(4,128)}, u32[]{:S(2)}) copy-start(f32[1,4,4096]{2,1,0:T(4,128)} %constant.75.clone.1) | copy-start | bytes 196612
  84.8 12.9 %collective-permute-start = (f32[4,4096]{1,0:T(4,128)S(1)}, f32[4,4096]{1,0:T(4,128)S(1)}, u32[]{:S(2)}, u32[]{:S(2)}) collective-permute-start(f32[4,4096]{1,0:T(4,128)S(1)} %get-tuple-element.160), channel_id=1, source_target_pairs={{1,0},{2,1},{3,2},{4,3},{5,4},{6,5},{7,6},{8,7},{9,8},{10,9},{11,1... | collective-permute-start | bytes 196616 | tf_op jit(solution)/shard_map/ppermute | solution.py:10
  105.2 21.0 %all-to-all-start.1 = ((f32[32,1,256]{2,1,0:T(1,128)}), f32[32,1,256]{2,1,0:T(1,128)S(1)}, u32[]{:S(2)}, u32[]{:S(2)}) async-start(f32[32,1,256]{2,1,0:T(1,128)} %reshape.17010), calls=%async_computation.1 | async-start | bytes 65536 | tf_op jit(solution)/shard_map/all_to_all | solution.py:122
  126.2 14.0 %all-to-all-start.2 = ((f32[32,1,384]{2,1,0:T(1,128)}), f32[32,1,384]{2,1,0:T(1,128)S(1)}, u32[]{:S(2)}, u32[]{:S(2)}) async-start(f32[32,1,384]{2,1,0:T(1,128)} %reshape.17012), calls=%async_computation.2 | async-start | bytes 98304 | tf_op jit(solution)/shard_map/all_to_all | solution.py:121
  147.2 14.8 %all-to-all-start.3 = ((f32[32,1,512]{2,1,0:T(1,128)}), f32[32,1,512]{2,1,0:T(1,128)S(1)}, u32[]{:S(2)}, u32[]{:S(2)}) async-start(f32[32,1,512]{2,1,0:T(1,128)} %reshape.17014), calls=%async_computation.3 | async-start | bytes 131072 | tf_op jit(solution)/shard_map/all_to_all | solution.py:126
where the time goes:
time: 169 us; the launch traced here: 165 us
  other arithmetic  65.7 us (39%)
  starting transfers between devices  34.9 us (21%)
  local copies, waits for them, and re-layouts  26.8 us (16%)
  between operations  22.8 us (13%)
  waiting for transfers between devices  15.3 us (9%)
    div x1, other arithmetic, thomas_forward(): factor = upper_val / pivots  17.8 us
    sub x1, other arithmetic, thomas_forward(): pivots = lower_val + upper_val + spectral - lower_val * factor  17.6 us
    unnamed x88, local copies, waits for them, and re-layouts  17.6 us
    all_to_all x1, starting transfers between devices, per_device(): lax.all_to_all(right_items, 'gz', split_axis=3, concat_axis=0, tiled=True)  12.2 us
    unnamed x12, other arithmetic  11.9 us
    all_to_all x1, starting transfers between devices, per_device(): lax.all_to_all(source_field, 'modes', split_axis=2, concat_axis=3, tiled=...  10.2 us
    add x1, other arithmetic, thomas_backward(): result = partial_value + factor * behind  9.85 us
    all_to_all x1, waiting for transfers between devices, per_device(): lax.all_to_all(paired, 'gz', split_axis=0, concat_axis=3, tiled=True)  8.01 us
  transfers between devices with their start and end apart: 5, of which 3 were waited for; matrix products, arithmetic and copies ran while one was open for 37% of the time, Pallas kernels for 0%

commit v1 on v0

v1 whole, which is shorter than its diff:
```python
import functools

import jax
import jax.numpy as jnp
from jax import lax
from jax.experimental import pallas as pl
from jax.experimental.pallas import tpu as pltpu
from jax.sharding import PartitionSpec as P

MESH = pl.DeviceIdType.MESH
LANES = 128


def kernel(
    modes, parts,
    f_hbm, low_s, up_s, es_s, ep_ref,
    out_hbm,
    F, W, O, SAB, AB, CS, CR, GR, RS, XR, V, T, FAC, HQ, AL, GA, EI, LAM,
    load_sem, store_sem, y1_send, y1_recv, y2_send, y2_recv, c_send, c_recv, g_send, g_recv, r_send, r_recv,
):
    rows = F.shape[0]
    last = rows - 1
    step = parts // modes
    mi = lax.axis_index("modes")
    gi = lax.axis_index("gz")
    is_solver = lax.rem(gi, step) == 0
    my_block = gi // step

    load = pltpu.make_async_copy(f_hbm, F, load_sem)
    load.start()

    barrier = pltpu.get_barrier_semaphore()

    def signal_modes(r, _):
        pl.semaphore_signal(barrier, inc=1, device_id={"modes": lax.rem(mi + r, modes)}, device_id_type=MESH)
        return 0

    lax.fori_loop(1, modes, signal_modes, 0)

    @pl.when(is_solver)
    def _():
        def signal_all(r, _):
            pl.semaphore_signal(barrier, inc=1, device_id={"gz": lax.rem(gi + r, parts)}, device_id_type=MESH)
            return 0

        lax.fori_loop(1, parts, signal_all, 0)

    @pl.when(jnp.logical_not(is_solver))
    def _():
        def signal_solvers(j, _):
            pl.semaphore_signal(barrier, inc=1, device_id={"gz": j * step}, device_id_type=MESH)
            return 0

        lax.fori_loop(0, modes, signal_solvers, 0)

    low = [low_s[k] for k in range(rows)]
    up = [up_s[k] for k in range(rows)]
    low[0] = jnp.where(gi == 0, 0.0, low[0])
    up[last] = jnp.where(gi == parts - 1, 0.0, up[last])

    for b in range(2):
        LAM[:, pl.ds(b, 1), :] = (es_s[mi * 2 + b] + ep_ref[...]).reshape(modes, 1, LANES)
    lam = LAM[...]
    excess = lam + low[0]
    for k in range(last):
        inv = 1.0 / (up[k] + excess)
        factor = up[k] * inv
        if k == 0:
            qv = low[0] * inv
            qh = lam * inv
        else:
            qv = (low[k] * inv) * qv
            qh = (lam + low[k] * qh) * inv
        FAC[k] = factor
        V[k] = qv
        HQ[k] = qh
        excess = lam + low[k + 1] * (excess * inv)
    v, t, h = qv, factor, qh
    T[last - 1] = t
    CS[:, 0] = low[last] * v
    CS[:, 1] = lam + low[last] * h
    for k in range(last - 2, -1, -1):
        factor = FAC[k]
        v = V[k] + factor * v
        t = factor * t
        h = HQ[k] + factor * h
        V[k] = v
        T[k] = t
    CS[:, 2] = t
    CS[:, 3] = h
    CS[:, 4] = jnp.full_like(t, 1.0) * up[last]

    for j in range(modes):
        for b in range(2):
            LAM[j, pl.ds(b, 1), :] = es_s[2 * j + b] + ep_ref[pl.ds(mi, 1), :]
    lam = LAM[...]
    load.wait()
    excess = lam + low[0]
    q = [None, None]
    for k in range(last):
        inv = 1.0 / (up[k] + excess)
        FAC[k] = up[k] * inv
        for c in range(2):
            q[c] = (F[k, c] if k == 0 else F[k, c] + low[k] * q[c]) * inv
            F[k, c] = q[c]
        excess = lam + low[k + 1] * (excess * inv)
    for c in range(2):
        SAB[c] = F[last, c] + low[last] * q[c]
    for k in range(last - 2, -1, -1):
        factor = FAC[k]
        for c in range(2):
            q[c] = F[k, c] + factor * q[c]
            if k:
                F[k, c] = q[c]
            else:
                SAB[2 + c] = q[c]

    pl.semaphore_wait(barrier, jnp.where(is_solver, modes - 1 + parts - 1, modes - 1 + modes))

    def y1_copy(target, slot):
        return pltpu.make_async_remote_copy(
            src_ref=SAB.at[:, target], dst_ref=AB.at[:, slot],
            send_sem=y1_send.at[target], recv_sem=y1_recv.at[slot],
            device_id={"modes": target}, device_id_type=MESH)

    def y2_copy(target, slot):
        return pltpu.make_async_remote_copy(
            src_ref=F.at[pl.ds(1, last - 1), :, target], dst_ref=W.at[:, :, slot],
            send_sem=y2_send.at[target], recv_sem=y2_recv.at[slot],
            device_id={"modes": target}, device_id_type=MESH)

    def c_copy(block, slot):
        return pltpu.make_async_remote_copy(
            src_ref=CS.at[block], dst_ref=CR.at[slot],
            send_sem=c_send.at[block], recv_sem=c_recv.at[slot],
            device_id={"gz": block * step}, device_id_type=MESH)

    def g_copy(block, slot):
        return pltpu.make_async_remote_copy(
            src_ref=AB.at[:, block], dst_ref=GR.at[slot],
            send_sem=g_send.at[block], recv_sem=g_recv.at[slot],
            device_id={"gz": block * step}, device_id_type=MESH)

    def r_copy(part, slot):
        return pltpu.make_async_remote_copy(
            src_ref=RS.at[part], dst_ref=XR.at[slot],
            send_sem=r_send.at[part], recv_sem=r_recv.at[slot],
            device_id={"gz": part}, device_id_type=MESH)

    def spread(i):
        half = modes // 2
        return jnp.where(lax.rem(i, 2) == 0, half + i // 2, half - (i + 1) // 2)

    def start_y1(i, _):
        y1_copy(lax.rem(mi + spread(i), modes), mi).start()
        return 0

    def start_y2(i, _):
        y2_copy(lax.rem(mi + spread(i), modes), mi).start()
        return 0

    def start_c(j, _):
        @pl.when(j * step != gi)
        def _():
            c_copy(j, gi).start()

        return 0

    lax.fori_loop(0, modes - 1, start_y1, 0)
    lax.fori_loop(0, modes, start_c, 0)
    lax.fori_loop(0, modes - 1, start_y2, 0)

    AB[:, mi] = SAB[:, mi]
    W[:, :, mi] = F[1:last, :, mi]

    @pl.when(is_solver)
    def _():
        CR[gi] = CS[my_block]

    def forward(i, _):
        block = lax.rem(mi + i, modes)

        @pl.when(i > 0)
        def _():
            y1_copy(block, block).wait_recv()

        @pl.when(block * step != gi)
        def _():
            g_copy(block, gi).start()

        @pl.when(block * step == gi)
        def _():
            GR[gi] = AB[:, block]

        return 0

    lax.fori_loop(0, modes, forward, 0)

    def up_by(x, d, fill):
        return jnp.concatenate([x[d:], jnp.full((d,) + x.shape[1:], fill, x.dtype)], axis=0)

    def down_by(x, d, fill):
        return jnp.concatenate([jnp.full((d,) + x.shape[1:], fill, x.dtype), x[:-d]], axis=0)

    @pl.when(is_solver)
    def _():
        def wait_c(i, _):
            c_copy(my_block, lax.rem(gi + i, parts)).wait_recv()
            return 0

        lax.fori_loop(1, parts, wait_c, 0)
        a = CR[:, 0]
        u = CR[:, 4]
        c = u * up_by(CR[:, 2], 1, 0.0)
        e = CR[:, 1] + u * up_by(CR[:, 3], 1, 0.0)
        d, level = 1, 0
        while d < parts:
            inv = 1.0 / (a + c + e)
            alpha = a * down_by(inv, d, 0.0)
            gamma = c * up_by(inv, d, 0.0)
            AL[level] = alpha
            GA[level] = gamma
            e = e + alpha * down_by(e, d, 0.0) + gamma * up_by(e, d, 0.0)
            a = alpha * down_by(a, d, 0.0)
            c = gamma * up_by(c, d, 0.0)
            d, level = 2 * d, level + 1
        EI[...] = 1.0 / e

        def wait_g(i, _):
            g_copy(my_block, lax.rem(gi + i, parts)).wait_recv()
            return 0

        lax.fori_loop(1, parts, wait_g, 0)
        for p in range(2):
            x = GR[:, p] + u * up_by(GR[:, 2 + p], 1, 0.0)
            d, level = 1, 0
            while d < parts:
                x = x + AL[level] * down_by(x, d, 0.0) + GA[level] * up_by(x, d, 0.0)
                d, level = 2 * d, level + 1
            x = x * EI[...]
            RS[:, 1, p] = x
            RS[:, 0, p] = down_by(x, 1, 0.0)

        def start_r(i, _):
            r_copy(lax.rem(gi + i, parts), my_block).start()
            return 0

        lax.fori_loop(1, parts, start_r, 0)
        XR[my_block] = RS[gi]

    def wait_y2(i, _):
        slot = lax.rem(mi + i, modes)
        y2_copy(slot, slot).wait_recv()
        return 0

    lax.fori_loop(1, modes, wait_y2, 0)

    def wait_r(j, _):
        @pl.when(j * step != gi)
        def _():
            r_copy(gi, j).wait_recv()

        return 0

    lax.fori_loop(0, modes, wait_r, 0)

    for p in range(2):
        prev = XR[:, 0, p]
        own = XR[:, 1, p]
        O[last, p] = own
        O[0, p] = AB[2 + p] + V[0] * prev + T[0] * own
        for k in range(1, last):
            O[k, p] = W[k - 1, p] + V[k] * prev + T[k] * own

    def store(j):
        return pltpu.make_async_copy(
            O.at[:, :, j], out_hbm.at[:, :, :, pl.ds(pl.multiple_of(j * LANES, LANES), LANES)], store_sem.at[j])

    def start_store(j, _):
        store(j).start()
        return 0

    lax.fori_loop(0, modes, start_store, 0)

    def finish_modes(i, _):
        target = lax.rem(mi + i, modes)
        y1_copy(target, target).wait_send()
        y2_copy(target, target).wait_send()
        return 0

    lax.fori_loop(1, modes, finish_modes, 0)

    def finish_solvers(j, _):
        @pl.when(j * step != gi)
        def _():
            c_copy(j, gi).wait_send()
            g_copy(j, gi).wait_send()

        return 0

    lax.fori_loop(0, modes, finish_solvers, 0)

    @pl.when(is_solver)
    def _():
        def finish_r(i, _):
            part = lax.rem(gi + i, parts)
            r_copy(part, my_block).wait_send()
            return 0

        lax.fori_loop(1, parts, finish_r, 0)

    def finish_store(j, _):
        store(j).wait()
        return 0

    lax.fori_loop(0, modes, finish_store, 0)


def solution(mesh):
    modes, parts = mesh.shape["modes"], mesh.shape["gz"]

    def per_device(source_field, coupling_below, coupling_above, eigen_stream, eigen_span):
        rows, _, kx, _ = source_field.shape
        levels = (parts - 1).bit_length()
        f32 = jnp.float32
        tile = (2, LANES)
        vmem = lambda *shape: pltpu.VMEM(shape + tile, f32)
        dma = lambda *shape: pltpu.SemaphoreType.DMA(shape)
        return pl.pallas_call(
            functools.partial(kernel, modes, parts),
            out_shape=jax.ShapeDtypeStruct((rows, 2, kx // modes, modes * LANES), f32),
            in_specs=[
                pl.BlockSpec(memory_space=pl.ANY),
                pl.BlockSpec(memory_space=pltpu.SMEM),
                pl.BlockSpec(memory_space=pltpu.SMEM),
                pl.BlockSpec(memory_space=pltpu.SMEM),
                pl.BlockSpec(memory_space=pltpu.VMEM),
            ],
            out_specs=pl.BlockSpec(memory_space=pl.ANY),
            scratch_shapes=[
                vmem(rows, 2, modes), vmem(rows - 2, 2, modes), vmem(rows, 2, modes),
                vmem(4, modes), vmem(4, modes),
                vmem(modes, 5), vmem(parts, 5), vmem(parts, 4), vmem(parts, 2, 2), vmem(modes, 2, 2),
                vmem(rows - 1, modes), vmem(rows - 1, modes), vmem(rows - 1, modes), vmem(rows - 1, modes),
                vmem(levels, parts), vmem(levels, parts), vmem(parts), vmem(modes),
                dma(), dma(modes), dma(modes), dma(modes), dma(modes), dma(modes),
                dma(modes), dma(parts), dma(modes), dma(parts), dma(parts), dma(modes),
            ],
            compiler_params=pltpu.CompilerParams(collective_id=0, has_side_effects=True),
        )(
            source_field.reshape(rows, 2, modes, 2, LANES),
            coupling_below, coupling_above, eigen_stream, eigen_span.reshape(modes, LANES),
        )

    return jax.shard_map(
        per_device,
        mesh=mesh,
        in_specs=(P("gz", None, None, "modes"), P("gz"), P("gz"), P(), P()),
        out_specs=P("gz", None, "modes", None),
        check_vma=False,
    )
```

time: 169 us -> 39.6 us (0.23)
  the two profiles are of different devices: /device:TPU:1 before, /device:TPU:24 now
where the time goes in v1:
time: 39.6 us; the launch traced here: 39.4 us
  Pallas kernels  37.5 us (95%)
  local copies, waits for them, and re-layouts  1.88 us (5%)
    pallas_call x1, Pallas kernels, per_device(): pl.pallas_call(functools.partial(kernel, modes, parts), out_shape=jax.Sha...  37.5 us
    unnamed x1, local copies, waits for them, and re-layouts  1.88 us

profile of v1, /device:TPU:24, one launch (start us, length us, event | category | flops | bytes accessed | tf_op | source)
XLA Modules:
  0.0 39.4 jit_solution(9457438838494231830)
XLA Ops:
  0.0 37.5 %shard_map.55 = f32[16,2,2,2048]{3,2,1,0:T(2,128)} custom-call(f32[16,2,16,2,128]{4,3,2,1,0:T(2,128)} %bitcast.2, f32[16]{0:T(128)} %low_s.1, f32[16]{0:T(128)} %up_s.1, f32[32]{0:T(128)} %es_s.1, f32[16,128]{1,0:T(8,128)} %bitcast.3), custom_call_target="tpu_custom_call" | custom-call | tf_op jit(solution)/shard_map/pallas_call | solution.py:329
  37.5 1.9 %copy.7 = f32[16,2,2,2048]{3,2,1,0:T(2,128)} copy(f32[16,2,2,2048]{3,2,1,0:T(2,128)} %shard_map.55) | data formatting | bytes 1048576

commit v2 on v1

v2 whole, which is shorter than its diff:
```python
import functools

import jax
import jax.numpy as jnp
from jax import lax
from jax.experimental import pallas as pl
from jax.experimental.pallas import tpu as pltpu
from jax.sharding import PartitionSpec as P

MESH = pl.DeviceIdType.MESH
LANES = 128


def gz_columns(parts):
    return min(4, parts // 2)


def spread(i, half):
    return jnp.where(lax.rem(i, 2) == 0, half + i // 2, half - (i + 1) // 2)


def exchange_kernel(
    modes, parts,
    f_hbm, low_hbm, up_hbm, es_hbm, ep_hbm,
    W, XR, V, T,
    F, SAB, CS, CR, GR, RS, FAC, HQ, AL, GA, EI, LAM, EP, low_s, up_s, es_s,
    load_sem, y_send, y_recv, ab_send, ab_recv, c_send, c_recv, r_send, r_recv,
):
    rows = F.shape[0]
    last = rows - 1
    half = modes // 4
    cols = gz_columns(parts)
    depth = parts // cols
    mi = lax.axis_index("modes")
    gi = lax.axis_index("gz")

    def home(j):
        d = j // 2 - half
        r = jnp.where(d > 0, 2 * d, jnp.where(d < 0, -2 * d - 1, 0)) * 2 + lax.rem(j, 2)
        return lax.rem(r, cols) * depth + r // cols

    rank = lax.rem(gi, depth) * cols + gi // depth
    is_solver = rank < modes
    my_block = spread(jnp.minimum(rank, modes - 1) // 2, half) * 2 + lax.rem(rank, 2)
    my_home = home(mi)

    loads = [
        pltpu.make_async_copy(src, dst, load_sem.at[i])
        for i, (src, dst) in enumerate(
            [(f_hbm, F), (low_hbm, low_s), (up_hbm, up_s), (es_hbm, es_s), (ep_hbm, EP)])
    ]
    for copy in loads:
        copy.start()

    barrier = pltpu.get_barrier_semaphore()

    def signal_modes(r, _):
        pl.semaphore_signal(barrier, inc=1, device_id={"modes": lax.rem(mi + r, modes)}, device_id_type=MESH)
        return 0

    lax.fori_loop(1, modes, signal_modes, 0)

    @pl.when(is_solver)
    def _():
        def signal_parts(r, _):
            part = lax.rem(gi + r, parts)
            pl.semaphore_signal(barrier, inc=1, device_id={"gz": part}, device_id_type=MESH)
            pl.semaphore_signal(barrier, inc=1, device_id={"modes": my_block, "gz": part}, device_id_type=MESH)
            return 0

        lax.fori_loop(1, parts, signal_parts, 0)

        @pl.when(my_block != mi)
        def _():
            pl.semaphore_signal(barrier, inc=1, device_id={"modes": my_block}, device_id_type=MESH)

    for copy in loads[1:]:
        copy.wait()
    low = [low_s[k] for k in range(rows)]
    up = [up_s[k] for k in range(rows)]
    low[0] = jnp.where(gi == 0, 0.0, low[0])
    up[last] = jnp.where(gi == parts - 1, 0.0, up[last])

    for j in range(modes):
        for b in range(2):
            LAM[j, pl.ds(b, 1), :] = es_s[2 * j + b] + EP[pl.ds(mi, 1), :]
    lam = LAM[...]
    loads[0].wait()
    excess = lam + low[0]
    q = [None, None]
    for k in range(last):
        inv = 1.0 / (up[k] + excess)
        FAC[k] = up[k] * inv
        for c in range(2):
            q[c] = (F[k, c] if k == 0 else F[k, c] + low[k] * q[c]) * inv
            F[k, c] = q[c]
        excess = lam + low[k + 1] * (excess * inv)
    for c in range(2):
        SAB[c] = F[last, c] + low[last] * q[c]
    for k in range(last - 2, -1, -1):
        factor = FAC[k]
        for c in range(2):
            q[c] = F[k, c] + factor * q[c]
            F[k, c] = q[c]
    for c in range(2):
        SAB[2 + c] = q[c]

    def ab_copy(target, slot):
        return pltpu.make_async_remote_copy(
            src_ref=SAB.at[:, target], dst_ref=GR.at[slot],
            send_sem=ab_send.at[target], recv_sem=ab_recv.at[slot],
            device_id={"modes": target, "gz": my_home}, device_id_type=MESH)

    def y_copy(target, slot):
        return pltpu.make_async_remote_copy(
            src_ref=F.at[pl.ds(0, last), :, target], dst_ref=W.at[:, :, slot],
            send_sem=y_send.at[target], recv_sem=y_recv.at[slot],
            device_id={"modes": target}, device_id_type=MESH)

    def c_copy(block, slot):
        return pltpu.make_async_remote_copy(
            src_ref=CS.at[block], dst_ref=CR.at[slot],
            send_sem=c_send.at[block], recv_sem=c_recv.at[slot],
            device_id={"gz": home(block)}, device_id_type=MESH)

    def r_copy(part, slot):
        return pltpu.make_async_remote_copy(
            src_ref=RS.at[part], dst_ref=XR.at[slot],
            send_sem=r_send.at[part], recv_sem=r_recv.at[slot],
            device_id={"gz": part}, device_id_type=MESH)

    solver_i = jnp.where(is_solver, 1, 0)
    home_i = jnp.where(my_home == gi, 1, 0)
    pl.semaphore_wait(barrier, (modes - 1) + (modes - home_i) + (modes - solver_i))

    def start_ab(i, _):
        target = lax.rem(mi + spread(i, modes // 2), modes)

        @pl.when(jnp.logical_or(target != mi, my_home != gi))
        def _():
            ab_copy(target, gi).start()

        return 0

    lax.fori_loop(0, modes, start_ab, 0)

    def start_y(i, _):
        y_copy(lax.rem(mi + spread(i, modes // 2), modes), mi).start()
        return 0

    lax.fori_loop(0, modes - 1, start_y, 0)
    W[:, :, mi] = F[0:last, :, mi]

    @pl.when(my_home == gi)
    def _():
        GR[gi] = SAB[:, mi]

    for b in range(2):
        LAM[:, pl.ds(b, 1), :] = (es_s[mi * 2 + b] + EP[...]).reshape(modes, 1, LANES)
    lam = LAM[...]
    excess = lam + low[0]
    for k in range(last):
        inv = 1.0 / (up[k] + excess)
        factor = up[k] * inv
        if k == 0:
            qv = low[0] * inv
            qh = lam * inv
        else:
            qv = (low[k] * inv) * qv
            qh = (lam + low[k] * qh) * inv
        FAC[k] = factor
        V[k] = qv
        HQ[k] = qh
        excess = lam + low[k + 1] * (excess * inv)
    v, t, h = qv, factor, qh
    T[last - 1] = t
    CS[:, 0] = low[last] * v
    CS[:, 1] = lam + low[last] * h
    for k in range(last - 2, -1, -1):
        factor = FAC[k]
        v = V[k] + factor * v
        t = factor * t
        h = HQ[k] + factor * h
        V[k] = v
        T[k] = t
    CS[:, 2] = t
    CS[:, 3] = h
    CS[:, 4] = jnp.full_like(t, 1.0) * up[last]

    def start_c(j, _):
        @pl.when(home(j) != gi)
        def _():
            c_copy(j, gi).start()

        return 0

    lax.fori_loop(0, modes, start_c, 0)

    def up_by(x, d, fill):
        return jnp.concatenate([x[d:], jnp.full((d,) + x.shape[1:], fill, x.dtype)], axis=0)

    def down_by(x, d, fill):
        return jnp.concatenate([jnp.full((d,) + x.shape[1:], fill, x.dtype), x[:-d]], axis=0)

    @pl.when(is_solver)
    def _():
        CR[gi] = CS[my_block]

        def wait_c(i, _):
            c_copy(my_block, lax.rem(gi + i, parts)).wait_recv()
            return 0

        lax.fori_loop(1, parts, wait_c, 0)
        a = CR[:, 0]
        u = CR[:, 4]
        c = u * up_by(CR[:, 2], 1, 0.0)
        e = CR[:, 1] + u * up_by(CR[:, 3], 1, 0.0)
        d, level = 1, 0
        while d < parts:
            inv = 1.0 / (a + c + e)
            alpha = a * down_by(inv, d, 0.0)
            gamma = c * up_by(inv, d, 0.0)
            AL[level] = alpha
            GA[level] = gamma
            e = e + alpha * down_by(e, d, 0.0) + gamma * up_by(e, d, 0.0)
            a = alpha * down_by(a, d, 0.0)
            c = gamma * up_by(c, d, 0.0)
            d, level = 2 * d, level + 1
        EI[...] = 1.0 / e

        def wait_ab(part, _):
            @pl.when(jnp.logical_or(my_block != mi, part != gi))
            def _():
                ab_copy(mi, part).wait_recv()

            return 0

        lax.fori_loop(0, parts, wait_ab, 0)
        for p in range(2):
            x = GR[:, p] + u * up_by(GR[:, 2 + p], 1, 0.0)
            d, level = 1, 0
            while d < parts:
                x = x + AL[level] * down_by(x, d, 0.0) + GA[level] * up_by(x, d, 0.0)
                d, level = 2 * d, level + 1
            x = x * EI[...]
            RS[:, 1, p] = x
            RS[:, 0, p] = down_by(x, 1, 0.0)

        def start_r(i, _):
            part = lax.rem(i, cols) * depth + i // cols

            @pl.when(part != gi)
            def _():
                r_copy(part, my_block).start()

            return 0

        lax.fori_loop(0, parts, start_r, 0)
        XR[my_block] = RS[gi]

    def wait_y(i, _):
        slot = lax.rem(mi + i, modes)
        y_copy(slot, slot).wait_recv()
        return 0

    lax.fori_loop(1, modes, wait_y, 0)

    def finish_modes(i, _):
        target = lax.rem(mi + i, modes)
        y_copy(target, target).wait_send()
        return 0

    lax.fori_loop(1, modes, finish_modes, 0)

    def finish_solvers(j, _):
        @pl.when(jnp.logical_or(j != mi, my_home != gi))
        def _():
            ab_copy(j, gi).wait_send()

        @pl.when(home(j) != gi)
        def _():
            c_copy(j, gi).wait_send()

        return 0

    lax.fori_loop(0, modes, finish_solvers, 0)

    @pl.when(is_solver)
    def _():
        def finish_r(i, _):
            r_copy(lax.rem(gi + i, parts), my_block).wait_send()
            return 0

        lax.fori_loop(1, parts, finish_r, 0)

    def wait_r(j, _):
        @pl.when(home(j) != gi)
        def _():
            r_copy(gi, j).wait_recv()

        return 0

    lax.fori_loop(0, modes, wait_r, 0)


def combine_kernel(W, XR, V, T, out_hbm, O, store_sem):
    rows, modes = O.shape[0], V.shape[1]
    last = rows - 1
    stores = [pltpu.make_async_copy(O.at[k], out_hbm.at[k], store_sem.at[k]) for k in range(rows)]
    for k in range(rows):
        for p in range(2):
            own = XR[:, 1, p]
            value = own if k == last else W[k, p] + V[k] * XR[:, 0, p] + T[k] * own
            for j in range(modes):
                O[k, p, :, pl.ds(j * LANES, LANES)] = value[j]
        stores[k].start()
    for copy in stores:
        copy.wait()


def solution(mesh):
    modes, parts = mesh.shape["modes"], mesh.shape["gz"]

    def per_device(source_field, coupling_below, coupling_above, eigen_stream, eigen_span):
        rows, _, kx, _ = source_field.shape
        levels = (parts - 1).bit_length()
        f32 = jnp.float32
        tile = (2, LANES)
        vmem = lambda *shape: pltpu.VMEM(shape + tile, f32)
        dma = lambda *shape: pltpu.SemaphoreType.DMA(shape)
        smem = lambda n: pltpu.SMEM((n,), f32)
        anywhere = pl.BlockSpec(memory_space=pl.ANY)
        local = pl.BlockSpec(memory_space=pltpu.VMEM)
        arrived = pl.pallas_call(
            functools.partial(exchange_kernel, modes, parts),
            out_shape=[
                vmem(rows - 1, 2, modes), vmem(modes, 2, 2), vmem(rows - 1, modes), vmem(rows - 1, modes),
            ],
            in_specs=[anywhere] * 5,
            out_specs=[local] * 4,
            scratch_shapes=[
                vmem(rows, 2, modes),
                vmem(4, modes), vmem(modes, 5), vmem(parts, 5), vmem(parts, 4), vmem(parts, 2, 2),
                vmem(rows - 1, modes), vmem(rows - 1, modes),
                vmem(levels, parts), vmem(levels, parts), vmem(parts), vmem(modes),
                pltpu.VMEM((modes, LANES), f32), smem(rows), smem(rows), smem(kx),
                dma(5), dma(modes), dma(modes), dma(modes), dma(parts), dma(modes), dma(parts), dma(parts), dma(modes),
            ],
            compiler_params=pltpu.CompilerParams(collective_id=0, has_side_effects=True),
        )(
            source_field.reshape(rows, 2, modes, 2, LANES),
            coupling_below, coupling_above, eigen_stream, eigen_span.reshape(modes, LANES),
        )
        return pl.pallas_call(
            combine_kernel,
            out_shape=jax.ShapeDtypeStruct((rows, 2, kx // modes, modes * LANES), f32),
            in_specs=[local] * 4,
            out_specs=anywhere,
            scratch_shapes=[pltpu.VMEM((rows, 2, kx // modes, modes * LANES), f32), dma(rows)],
            compiler_params=pltpu.CompilerParams(vmem_limit_bytes=4 << 20),
        )(*[pltpu.with_memory_space_constraint(x, pltpu.VMEM) for x in arrived])

    return jax.shard_map(
        per_device,
        mesh=mesh,
        in_specs=(P("gz", None, None, "modes"), P("gz"), P("gz"), P(), P()),
        out_specs=P("gz", None, "modes", None),
        check_vma=False,
    )
```

time: 39.6 us -> 33.8 us (0.85)
  the two profiles are of different devices: /device:TPU:24 before, /device:TPU:1 now
where the time goes in v2:
time: 33.8 us; the launch traced here: 33.7 us
  Pallas kernels  33.7 us (100%)
    pallas_call x1, Pallas kernels, per_device(): pl.pallas_call(functools.partial(exchange_kernel, modes, parts), out_shap...  32.5 us
    pallas_call x1, Pallas kernels, per_device(): pl.pallas_call(combine_kernel, out_shape=jax.ShapeDtypeStruct((rows, 2, k...  1.19 us

profile of v2, /device:TPU:1, one launch (start us, length us, event | category | flops | bytes accessed | tf_op | source)
XLA Modules:
  0.0 33.7 jit_solution(15475949079089990285)
XLA Ops:
  0.0 32.5 %shard_map.55 = (f32[15,2,16,2,128]{4,3,2,1,0:T(2,128)S(1)}, f32[16,2,2,2,128]{4,3,2,1,0:T(2,128)S(1)}, f32[15,16,2,128]{3,2,1,0:T(2,128)S(1)}, f32[15,16,2,128]{3,2,1,0:T(2,128)S(1)}) custom-call(f32[16,2,16,2,128]{4,3,2,1,0:T(2,128)} %bitcast.2, f32[16]{0:T(128)} %low_hbm.1, f32[16]{0:T(128)} %up_hbm.1, f32[32]{0:T(128)} %es_hbm.1, f32[16,128]{1,0:T(8,128)} %bitcast.3), custom_call_target="tpu_custom_call" | custom-call | tf_op jit(solution)/shard_map/pallas_call | solution.py:334
  32.5 1.2 %shard_map.56 = f32[16,2,2,2048]{3,2,1,0:T(2,128)} custom-call(f32[15,2,16,2,128]{4,3,2,1,0:T(2,128)S(1)} %get-tuple-element.9.W, f32[16,2,2,2,128]{4,3,2,1,0:T(2,128)S(1)} %get-tuple-element.10.XR, f32[15,16,2,128]{3,2,1,0:T(2,128)S(1)} %get-tuple-element.11.V, f32[15,16,2,128]{3,2,1,0:T(2,128)S(1)} %get-tuple-element.12.T), custom_call_target="tpu_custom_call" | custom-call | tf_op jit(solution)/shard_map/pallas_call | solution.py:354

commit v3 on v2

--- a/solution.py
+++ b/solution.py
@@ -23,8 +23,8 @@
     modes, parts,
     f_hbm, low_hbm, up_hbm, es_hbm, ep_hbm,
     W, XR, V, T,
-    F, SAB, CS, CR, GR, RS, FAC, HQ, AL, GA, EI, LAM, EP, low_s, up_s, es_s,
-    load_sem, y_send, y_recv, ab_send, ab_recv, c_send, c_recv, r_send, r_recv,
+    F, SAB, AB, CS, CR, GR, RS, FAC, AL, GA, EI, PK, LAM, EP, low_s, up_s, es_s,
+    load_sem, y_send, y_recv, s_send, s_recv, ab_send, ab_recv, c_send, c_recv, r_send, r_recv,
 ):
     rows = F.shape[0]
     last = rows - 1
@@ -43,6 +43,7 @@
     is_solver = rank < modes
     my_block = spread(jnp.minimum(rank, modes - 1) // 2, half) * 2 + lax.rem(rank, 2)
     my_home = home(mi)
+    is_late = lax.rem(gi, depth) >= depth // 2
 
     loads = [
         pltpu.make_async_copy(src, dst, load_sem.at[i])
@@ -65,14 +66,14 @@
         def signal_parts(r, _):
             part = lax.rem(gi + r, parts)
             pl.semaphore_signal(barrier, inc=1, device_id={"gz": part}, device_id_type=MESH)
-            pl.semaphore_signal(barrier, inc=1, device_id={"modes": my_block, "gz": part}, device_id_type=MESH)
+
+            @pl.when(lax.rem(part, depth) >= depth // 2)
+            def _():
+                pl.semaphore_signal(barrier, inc=1, device_id={"modes": my_block, "gz": part}, device_id_type=MESH)
+
             return 0
 
         lax.fori_loop(1, parts, signal_parts, 0)
-
-        @pl.when(my_block != mi)
-        def _():
-            pl.semaphore_signal(barrier, inc=1, device_id={"modes": my_block}, device_id_type=MESH)
 
     for copy in loads[1:]:
         copy.wait()
@@ -80,6 +81,13 @@
     up = [up_s[k] for k in range(rows)]
     low[0] = jnp.where(gi == 0, 0.0, low[0])
     up[last] = jnp.where(gi == parts - 1, 0.0, up[last])
+
+    lane = lax.broadcasted_iota(jnp.int32, (2, LANES), 1)
+    packed = jnp.zeros((2, LANES), jnp.float32)
+    for k in range(rows):
+        packed = jnp.where(lane == k, low[k], packed)
+        packed = jnp.where(lane == rows + k, up[k], packed)
+    CS[...] = packed
 
     for j in range(modes):
         for b in range(2):
@@ -105,7 +113,19 @@
     for c in range(2):
         SAB[2 + c] = q[c]
 
-    def ab_copy(target, slot):
+    def s_copy(target, slot):
+        return pltpu.make_async_remote_copy(
+            src_ref=SAB.at[:, target], dst_ref=AB.at[:, slot],
+            send_sem=s_send.at[target], recv_sem=s_recv.at[slot],
+            device_id={"modes": target}, device_id_type=MESH)
+
+    def forward_copy(block, slot):
+        return pltpu.make_async_remote_copy(
+            src_ref=AB.at[:, block], dst_ref=GR.at[slot],
+            send_sem=ab_send.at[block], recv_sem=ab_recv.at[slot],
+            device_id={"gz": home(block)}, device_id_type=MESH)
+
+    def direct_copy(target, slot):
         return pltpu.make_async_remote_copy(
             src_ref=SAB.at[:, target], dst_ref=GR.at[slot],
             send_sem=ab_send.at[target], recv_sem=ab_recv.at[slot],
@@ -119,7 +139,7 @@
 
     def c_copy(block, slot):
         return pltpu.make_async_remote_copy(
-            src_ref=CS.at[block], dst_ref=CR.at[slot],
+            src_ref=CS, dst_ref=CR.at[slot],
             send_sem=c_send.at[block], recv_sem=c_recv.at[slot],
             device_id={"gz": home(block)}, device_id_type=MESH)
 
@@ -130,19 +150,34 @@
             device_id={"gz": part}, device_id_type=MESH)
 
     solver_i = jnp.where(is_solver, 1, 0)
-    home_i = jnp.where(my_home == gi, 1, 0)
-    pl.semaphore_wait(barrier, (modes - 1) + (modes - home_i) + (modes - solver_i))
-
-    def start_ab(i, _):
-        target = lax.rem(mi + spread(i, modes // 2), modes)
-
-        @pl.when(jnp.logical_or(target != mi, my_home != gi))
+    late_i = jnp.where(is_late, modes, 0)
+    pl.semaphore_wait(barrier, (modes - 1) + (modes - solver_i) + late_i)
+
+    @pl.when(is_late)
+    def _():
+        def start_direct(i, _):
+            direct_copy(lax.rem(mi + spread(i, modes // 2), modes), gi).start()
+            return 0
+
+        lax.fori_loop(0, modes, start_direct, 0)
+
+    @pl.when(jnp.logical_not(is_late))
+    def _():
+        def start_s(i, _):
+            s_copy(lax.rem(mi + spread(i, modes // 2), modes), mi).start()
+            return 0
+
+        lax.fori_loop(0, modes - 1, start_s, 0)
+        AB[:, mi] = SAB[:, mi]
+
+    def start_c(j, _):
+        @pl.when(home(j) != gi)
         def _():
-            ab_copy(target, gi).start()
-
-        return 0
-
-    lax.fori_loop(0, modes, start_ab, 0)
+            c_copy(j, gi).start()
+
+        return 0
+
+    lax.fori_loop(0, modes, start_c, 0)
 
     def start_y(i, _):
         y_copy(lax.rem(mi + spread(i, modes // 2), modes), mi).start()
@@ -150,10 +185,6 @@
 
     lax.fori_loop(0, modes - 1, start_y, 0)
     W[:, :, mi] = F[0:last, :, mi]
-
-    @pl.when(my_home == gi)
-    def _():
-        GR[gi] = SAB[:, mi]
 
     for b in range(2):
         LAM[:, pl.ds(b, 1), :] = (es_s[mi * 2 + b] + EP[...]).reshape(modes, 1, LANES)
@@ -162,89 +193,118 @@
     for k in range(last):
         inv = 1.0 / (up[k] + excess)
         factor = up[k] * inv
-        if k == 0:
-            qv = low[0] * inv
-            qh = lam * inv
-        else:
-            qv = (low[k] * inv) * qv
-            qh = (lam + low[k] * qh) * inv
+        v = low[0] * inv if k == 0 else (low[k] * inv) * v
         FAC[k] = factor
-        V[k] = qv
-        HQ[k] = qh
+        V[k] = v
         excess = lam + low[k + 1] * (excess * inv)
-    v, t, h = qv, factor, qh
+    t = factor
     T[last - 1] = t
-    CS[:, 0] = low[last] * v
-    CS[:, 1] = lam + low[last] * h
     for k in range(last - 2, -1, -1):
         factor = FAC[k]
         v = V[k] + factor * v
         t = factor * t
-        h = HQ[k] + factor * h
         V[k] = v
         T[k] = t
-    CS[:, 2] = t
-    CS[:, 3] = h
-    CS[:, 4] = jnp.full_like(t, 1.0) * up[last]
-
-    def start_c(j, _):
-        @pl.when(home(j) != gi)
-        def _():
-            c_copy(j, gi).start()
-
-        return 0
-
-    lax.fori_loop(0, modes, start_c, 0)
-
-    def up_by(x, d, fill):
-        return jnp.concatenate([x[d:], jnp.full((d,) + x.shape[1:], fill, x.dtype)], axis=0)
-
-    def down_by(x, d, fill):
-        return jnp.concatenate([jnp.full((d,) + x.shape[1:], fill, x.dtype), x[:-d]], axis=0)
+
+    @pl.when(jnp.logical_not(is_late))
+    def _():
+        def forward(i, _):
+            block = lax.rem(mi + i, modes)
+
+            @pl.when(i > 0)
+            def _():
+                s_copy(block, block).wait_recv()
+
+            @pl.when(home(block) != gi)
+            def _():
+                forward_copy(block, gi).start()
+
+            @pl.when(home(block) == gi)
+            def _():
+                GR[gi] = AB[:, block]
+
+            return 0
+
+        lax.fori_loop(0, modes, forward, 0)
+
+    count = 2 * parts
+
+    def ahead(x, d):
+        return pltpu.roll(x, count - 2 * d, 0)
+
+    def behind(x, d):
+        return pltpu.roll(x, 2 * d, 0)
+
+    def spread_lane(x, k):
+        return jnp.broadcast_to(x[:, k:k + 1], (count, LANES))
 
     @pl.when(is_solver)
     def _():
-        CR[gi] = CS[my_block]
+        CR[gi] = CS[...]
 
         def wait_c(i, _):
             c_copy(my_block, lax.rem(gi + i, parts)).wait_recv()
             return 0
 
         lax.fori_loop(1, parts, wait_c, 0)
-        a = CR[:, 0]
-        u = CR[:, 4]
-        c = u * up_by(CR[:, 2], 1, 0.0)
-        e = CR[:, 1] + u * up_by(CR[:, 3], 1, 0.0)
+        PK[0] = CR[...].reshape(count, LANES)
+        couplings = PK[0]
+        odd = lax.rem(lax.broadcasted_iota(jnp.int32, (count, LANES), 0), 2) == 1
+        stream = jnp.where(odd, es_s[mi * 2 + 1], es_s[mi * 2])
+        lam = stream + jnp.broadcast_to(EP[pl.ds(my_block, 1), :], (count, LANES))
+        for k in range(last):
+            lo = spread_lane(couplings, k)
+            hi = spread_lane(couplings, rows + k)
+            excess = lam + lo if k == 0 else lam + lo * (excess * inv)
+            inv = 1.0 / (hi + excess)
+            factor = hi * inv
+            if k == 0:
+                v = lo * inv
+                qh = lam * inv
+                h = qh
+                t = factor
+            else:
+                v = (lo * inv) * v
+                qh = (lam + lo * qh) * inv
+                h = h + t * qh
+                t = t * factor
+        lo = spread_lane(couplings, last)
+        u = spread_lane(couplings, rows + last)
+        a = lo * v
+        c = u * ahead(t, 1)
+        e = lam + lo * qh + u * ahead(h, 1)
         d, level = 1, 0
         while d < parts:
             inv = 1.0 / (a + c + e)
-            alpha = a * down_by(inv, d, 0.0)
-            gamma = c * up_by(inv, d, 0.0)
+            alpha = a * behind(inv, d)
+            gamma = c * ahead(inv, d)
             AL[level] = alpha
             GA[level] = gamma
-            e = e + alpha * down_by(e, d, 0.0) + gamma * up_by(e, d, 0.0)
-            a = alpha * down_by(a, d, 0.0)
-            c = gamma * up_by(c, d, 0.0)
+            e = e + alpha * behind(e, d) + gamma * ahead(e, d)
+            a = alpha * behind(a, d)
+            c = gamma * ahead(c, d)
             d, level = 2 * d, level + 1
         EI[...] = 1.0 / e
 
         def wait_ab(part, _):
-            @pl.when(jnp.logical_or(my_block != mi, part != gi))
-            def _():
-                ab_copy(mi, part).wait_recv()
+            @pl.when(part != gi)
+            def _():
+                direct_copy(mi, part).wait_recv()
 
             return 0
 
         lax.fori_loop(0, parts, wait_ab, 0)
         for p in range(2):
-            x = GR[:, p] + u * up_by(GR[:, 2 + p], 1, 0.0)
+            PK[0] = GR[:, p].reshape(count, LANES)
+            PK[1] = GR[:, 2 + p].reshape(count, LANES)
+            x = PK[0] + u * ahead(PK[1], 1)
             d, level = 1, 0
             while d < parts:
-                x = x + AL[level] * down_by(x, d, 0.0) + GA[level] * up_by(x, d, 0.0)
+                x = x + AL[level] * behind(x, d) + GA[level] * ahead(x, d)
                 d, level = 2 * d, level + 1
             x = x * EI[...]
-            RS[:, 1, p] = x
-            RS[:, 0, p] = down_by(x, 1, 0.0)
+            RS[:, 1, p] = x.reshape(parts, 2, LANES)
+            RS[:, 0, p] = behind(x, 1).reshape(parts, 2, LANES)
 
         def start_r(i, _):
             part = lax.rem(i, cols) * depth + i // cols
@@ -273,17 +333,23 @@
     lax.fori_loop(1, modes, finish_modes, 0)
 
     def finish_solvers(j, _):
-        @pl.when(jnp.logical_or(j != mi, my_home != gi))
-        def _():
-            ab_copy(j, gi).wait_send()
-
         @pl.when(home(j) != gi)
         def _():
             c_copy(j, gi).wait_send()
+            forward_copy(j, gi).wait_send()
 
         return 0
 
     lax.fori_loop(0, modes, finish_solvers, 0)
+
+    @pl.when(jnp.logical_not(is_late))
+    def _():
+        def finish_s(i, _):
+            target = lax.rem(mi + i, modes)
+            s_copy(target, target).wait_send()
+            return 0
+
+        lax.fori_loop(1, modes, finish_s, 0)
 
     @pl.when(is_solver)
     def _():
@@ -327,6 +393,7 @@
         f32 = jnp.float32
         tile = (2, LANES)
         vmem = lambda *shape: pltpu.VMEM(shape + tile, f32)
+        flat = lambda *shape: pltpu.VMEM(shape + (2 * parts, LANES), f32)
         dma = lambda *shape: pltpu.SemaphoreType.DMA(shape)
         smem = lambda n: pltpu.SMEM((n,), f32)
         anywhere = pl.BlockSpec(memory_space=pl.ANY)
@@ -340,11 +407,12 @@
             out_specs=[local] * 4,
             scratch_shapes=[
                 vmem(rows, 2, modes),
-                vmem(4, modes), vmem(modes, 5), vmem(parts, 5), vmem(parts, 4), vmem(parts, 2, 2),
-                vmem(rows - 1, modes), vmem(rows - 1, modes),
-                vmem(levels, parts), vmem(levels, parts), vmem(parts), vmem(modes),
+                vmem(4, modes), vmem(4, modes), vmem(), vmem(parts), vmem(parts, 4), vmem(parts, 2, 2),
+                vmem(rows - 1, modes),
+                flat(levels), flat(levels), flat(), flat(2), vmem(modes),
                 pltpu.VMEM((modes, LANES), f32), smem(rows), smem(rows), smem(kx),
-                dma(5), dma(modes), dma(modes), dma(modes), dma(parts), dma(modes), dma(parts), dma(parts), dma(modes),
+                dma(5), dma(modes), dma(modes), dma(modes), dma(modes),
+                dma(modes), dma(parts), dma(modes), dma(parts), dma(parts), dma(modes),
             ],
             compiler_params=pltpu.CompilerParams(collective_id=0, has_side_effects=True),
         )(

time: 33.8 us -> 32.2 us (0.953); the launches traced: 33.7 us -> 31.7 us
  Pallas kernels: 33.7 us -> 31.7 us
    pallas_call x1, Pallas kernels: 32.5 us -> 30.5 us  [per_device(): pl.pallas_call(functools.partial(exchange_kernel, modes, parts), out_shap...]
where the time goes in v3:
time: 32.2 us; the launch traced here: 31.7 us
  Pallas kernels  31.7 us (98%)
    pallas_call x1, Pallas kernels, per_device(): pl.pallas_call(functools.partial(exchange_kernel, modes, parts), out_shap...  30.5 us
    pallas_call x1, Pallas kernels, per_device(): pl.pallas_call(combine_kernel, out_shape=jax.ShapeDtypeStruct((rows, 2, k...  1.19 us

profile of v3, /device:TPU:1, one launch (start us, length us, event | category | flops | bytes accessed | tf_op | source)
XLA Modules:
  0.0 31.7 jit_solution(1301830434460761140)
XLA Ops:
  0.0 30.5 %shard_map.55 = (f32[15,2,16,2,128]{4,3,2,1,0:T(2,128)S(1)}, f32[16,2,2,2,128]{4,3,2,1,0:T(2,128)S(1)}, f32[15,16,2,128]{3,2,1,0:T(2,128)S(1)}, f32[15,16,2,128]{3,2,1,0:T(2,128)S(1)}) custom-call(f32[16,2,16,2,128]{4,3,2,1,0:T(2,128)} %bitcast.2, f32[16]{0:T(128)} %low_hbm.1, f32[16]{0:T(128)} %up_hbm.1, f32[32]{0:T(128)} %es_hbm.1, f32[16,128]{1,0:T(8,128)} %bitcast.3), custom_call_target="tpu_custom_call" | custom-call | tf_op jit(solution)/shard_map/pallas_call | solution.py:401
  30.5 1.2 %shard_map.56 = f32[16,2,2,2048]{3,2,1,0:T(2,128)} custom-call(f32[15,2,16,2,128]{4,3,2,1,0:T(2,128)S(1)} %get-tuple-element.9.W, f32[16,2,2,2,128]{4,3,2,1,0:T(2,128)S(1)} %get-tuple-element.10.XR, f32[15,16,2,128]{3,2,1,0:T(2,128)S(1)} %get-tuple-element.11.V, f32[15,16,2,128]{3,2,1,0:T(2,128)S(1)} %get-tuple-element.12.T), custom_call_target="tpu_custom_call" | custom-call | tf_op jit(solution)/shard_map/pallas_call | solution.py:422

commit v4 on v3

--- a/solution.py
+++ b/solution.py
@@ -34,16 +34,25 @@
     mi = lax.axis_index("modes")
     gi = lax.axis_index("gz")
 
+    moved = (modes - 2, 4) if (modes, parts) == (16, 32) else None
+
     def home(j):
         d = j // 2 - half
         r = jnp.where(d > 0, 2 * d, jnp.where(d < 0, -2 * d - 1, 0)) * 2 + lax.rem(j, 2)
-        return lax.rem(r, cols) * depth + r // cols
+        site = lax.rem(r, cols) * depth + r // cols
+        return jnp.where(r == moved[0], moved[1], site) if moved else site
 
     rank = lax.rem(gi, depth) * cols + gi // depth
+    if moved:
+        rank = jnp.where(gi == moved[1], moved[0], jnp.where(rank == moved[0], modes, rank))
     is_solver = rank < modes
     my_block = spread(jnp.minimum(rank, modes - 1) // 2, half) * 2 + lax.rem(rank, 2)
     my_home = home(mi)
-    is_late = lax.rem(gi, depth) >= depth // 2
+    def late(part):
+        z_late = lax.rem(part, depth) >= depth // 2
+        return jnp.logical_and(z_late, part != moved[1]) if moved else z_late
+
+    is_late = late(gi)
 
     loads = [
         pltpu.make_async_copy(src, dst, load_sem.at[i])
@@ -67,7 +76,7 @@
             part = lax.rem(gi + r, parts)
             pl.semaphore_signal(barrier, inc=1, device_id={"gz": part}, device_id_type=MESH)
 
-            @pl.when(lax.rem(part, depth) >= depth // 2)
+            @pl.when(late(part))
             def _():
                 pl.semaphore_signal(barrier, inc=1, device_id={"modes": my_block, "gz": part}, device_id_type=MESH)
 
@@ -209,9 +218,10 @@
     @pl.when(jnp.logical_not(is_late))
     def _():
         def forward(i, _):
-            block = lax.rem(mi + i, modes)
-
-            @pl.when(i > 0)
+            r = modes - 1 - i
+            block = spread(r // 2, half) * 2 + lax.rem(r, 2)
+
+            @pl.when(block != mi)
             def _():
                 s_copy(block, block).wait_recv()
 

time: 32.2 us -> 31.9 us (level); the launches traced: 31.7 us -> 31.8 us
  no operation moved by 1% of the time
where the time goes in v4:
time: 31.9 us; the launch traced here: 31.8 us
  Pallas kernels  31.8 us (100%)
    pallas_call x1, Pallas kernels, per_device(): pl.pallas_call(functools.partial(exchange_kernel, modes, parts), out_shap...  30.6 us
    pallas_call x1, Pallas kernels, per_device(): pl.pallas_call(combine_kernel, out_shape=jax.ShapeDtypeStruct((rows, 2, k...  1.19 us

profile of v4, /device:TPU:1, one launch (start us, length us, event | category | flops | bytes accessed | tf_op | source)
XLA Modules:
  0.0 31.8 jit_solution(3180063374344751593)
XLA Ops:
  0.0 30.6 %shard_map.55 = (f32[15,2,16,2,128]{4,3,2,1,0:T(2,128)S(1)}, f32[16,2,2,2,128]{4,3,2,1,0:T(2,128)S(1)}, f32[15,16,2,128]{3,2,1,0:T(2,128)S(1)}, f32[15,16,2,128]{3,2,1,0:T(2,128)S(1)}) custom-call(f32[16,2,16,2,128]{4,3,2,1,0:T(2,128)} %bitcast.2, f32[16]{0:T(128)} %low_hbm.1, f32[16]{0:T(128)} %up_hbm.1, f32[32]{0:T(128)} %es_hbm.1, f32[16,128]{1,0:T(8,128)} %bitcast.3), custom_call_target="tpu_custom_call" | custom-call | tf_op jit(solution)/shard_map/pallas_call | solution.py:411
  30.6 1.2 %shard_map.56 = f32[16,2,2,2048]{3,2,1,0:T(2,128)} custom-call(f32[15,2,16,2,128]{4,3,2,1,0:T(2,128)S(1)} %get-tuple-element.9.W, f32[16,2,2,2,128]{4,3,2,1,0:T(2,128)S(1)} %get-tuple-element.10.XR, f32[15,16,2,128]{3,2,1,0:T(2,128)S(1)} %get-tuple-element.11.V, f32[15,16,2,128]{3,2,1,0:T(2,128)S(1)} %get-tuple-element.12.T), custom_call_target="tpu_custom_call" | custom-call | tf_op jit(solution)/shard_map/pallas_call | solution.py:432

commit v5 on v4

--- a/solution.py
+++ b/solution.py
@@ -192,7 +192,10 @@
         y_copy(lax.rem(mi + spread(i, modes // 2), modes), mi).start()
         return 0
 
-    lax.fori_loop(0, modes - 1, start_y, 0)
+    @pl.when(jnp.logical_not(is_late))
+    def _():
+        lax.fori_loop(0, modes - 1, start_y, 0)
+
     W[:, :, mi] = F[0:last, :, mi]
 
     for b in range(2):
@@ -214,6 +217,10 @@
         t = factor * t
         V[k] = v
         T[k] = t
+
+    @pl.when(is_late)
+    def _():
+        lax.fori_loop(0, modes - 1, start_y, 0)
 
     @pl.when(jnp.logical_not(is_late))
     def _():
@@ -382,14 +389,19 @@
 def combine_kernel(W, XR, V, T, out_hbm, O, store_sem):
     rows, modes = O.shape[0], V.shape[1]
     last = rows - 1
-    stores = [pltpu.make_async_copy(O.at[k], out_hbm.at[k], store_sem.at[k]) for k in range(rows)]
+    chunk = 4
+    stores = [
+        pltpu.make_async_copy(O.at[pl.ds(k, chunk)], out_hbm.at[pl.ds(k, chunk)], store_sem.at[k // chunk])
+        for k in range(0, rows, chunk)
+    ]
     for k in range(rows):
         for p in range(2):
             own = XR[:, 1, p]
             value = own if k == last else W[k, p] + V[k] * XR[:, 0, p] + T[k] * own
             for j in range(modes):
                 O[k, p, :, pl.ds(j * LANES, LANES)] = value[j]
-        stores[k].start()
+        if k % chunk == chunk - 1:
+            stores[k // chunk].start()
     for copy in stores:
         copy.wait()
 
@@ -434,7 +446,7 @@
             out_shape=jax.ShapeDtypeStruct((rows, 2, kx // modes, modes * LANES), f32),
             in_specs=[local] * 4,
             out_specs=anywhere,
-            scratch_shapes=[pltpu.VMEM((rows, 2, kx // modes, modes * LANES), f32), dma(rows)],
+            scratch_shapes=[pltpu.VMEM((rows, 2, kx // modes, modes * LANES), f32), dma(rows // 4)],
             compiler_params=pltpu.CompilerParams(vmem_limit_bytes=4 << 20),
         )(*[pltpu.with_memory_space_constraint(x, pltpu.VMEM) for x in arrived])
 

time: 31.9 us -> 31.8 us (level)
  no operation moved by 1% of the time
where the time goes in v5:
time: 31.8 us; the launch traced here: 31.7 us
  Pallas kernels  31.7 us (100%)
    pallas_call x1, Pallas kernels, per_device(): pl.pallas_call(functools.partial(exchange_kernel, modes, parts), out_shap...  30.6 us
    pallas_call x1, Pallas kernels, per_device(): pl.pallas_call(combine_kernel, out_shape=jax.ShapeDtypeStruct((rows, 2, k...  1.12 us

profile of v5, /device:TPU:1, one launch (start us, length us, event | category | flops | bytes accessed | tf_op | source)
XLA Modules:
  0.0 31.7 jit_solution(7400659041212100178)
XLA Ops:
  0.0 30.6 %shard_map.55 = (f32[15,2,16,2,128]{4,3,2,1,0:T(2,128)S(1)}, f32[16,2,2,2,128]{4,3,2,1,0:T(2,128)S(1)}, f32[15,16,2,128]{3,2,1,0:T(2,128)S(1)}, f32[15,16,2,128]{3,2,1,0:T(2,128)S(1)}) custom-call(f32[16,2,16,2,128]{4,3,2,1,0:T(2,128)} %bitcast.2, f32[16]{0:T(128)} %low_hbm.1, f32[16]{0:T(128)} %up_hbm.1, f32[32]{0:T(128)} %es_hbm.1, f32[16,128]{1,0:T(8,128)} %bitcast.3), custom_call_target="tpu_custom_call" | custom-call | tf_op jit(solution)/shard_map/pallas_call | solution.py:423
  30.6 1.1 %shard_map.56 = f32[16,2,2,2048]{3,2,1,0:T(2,128)} custom-call(f32[15,2,16,2,128]{4,3,2,1,0:T(2,128)S(1)} %get-tuple-element.9.W, f32[16,2,2,2,128]{4,3,2,1,0:T(2,128)S(1)} %get-tuple-element.10.XR, f32[15,16,2,128]{3,2,1,0:T(2,128)S(1)} %get-tuple-element.11.V, f32[15,16,2,128]{3,2,1,0:T(2,128)S(1)} %get-tuple-element.12.T), custom_call_target="tpu_custom_call" | custom-call | tf_op jit(solution)/shard_map/pallas_call | solution.py:444

commit v6 on v5

--- a/solution.py
+++ b/solution.py
@@ -389,7 +389,7 @@
 def combine_kernel(W, XR, V, T, out_hbm, O, store_sem):
     rows, modes = O.shape[0], V.shape[1]
     last = rows - 1
-    chunk = 4
+    chunk = 8
     stores = [
         pltpu.make_async_copy(O.at[pl.ds(k, chunk)], out_hbm.at[pl.ds(k, chunk)], store_sem.at[k // chunk])
         for k in range(0, rows, chunk)
@@ -446,7 +446,7 @@
             out_shape=jax.ShapeDtypeStruct((rows, 2, kx // modes, modes * LANES), f32),
             in_specs=[local] * 4,
             out_specs=anywhere,
-            scratch_shapes=[pltpu.VMEM((rows, 2, kx // modes, modes * LANES), f32), dma(rows // 4)],
+            scratch_shapes=[pltpu.VMEM((rows, 2, kx // modes, modes * LANES), f32), dma(rows // 8)],
             compiler_params=pltpu.CompilerParams(vmem_limit_bytes=4 << 20),
         )(*[pltpu.with_memory_space_constraint(x, pltpu.VMEM) for x in arrived])
 

time: 31.8 us -> 31.9 us (level)
  no operation moved by 1% of the time
where the time goes in v6:
time: 31.9 us; the launch traced here: 31.8 us
  Pallas kernels  31.8 us (100%)
    pallas_call x1, Pallas kernels, per_device(): pl.pallas_call(functools.partial(exchange_kernel, modes, parts), out_shap...  30.6 us
    pallas_call x1, Pallas kernels, per_device(): pl.pallas_call(combine_kernel, out_shape=jax.ShapeDtypeStruct((rows, 2, k...  1.15 us

profile of v6, /device:TPU:1, one launch (start us, length us, event | category | flops | bytes accessed | tf_op | source)
XLA Modules:
  0.0 31.8 jit_solution(15124684382859881831)
XLA Ops:
  0.0 30.6 %shard_map.55 = (f32[15,2,16,2,128]{4,3,2,1,0:T(2,128)S(1)}, f32[16,2,2,2,128]{4,3,2,1,0:T(2,128)S(1)}, f32[15,16,2,128]{3,2,1,0:T(2,128)S(1)}, f32[15,16,2,128]{3,2,1,0:T(2,128)S(1)}) custom-call(f32[16,2,16,2,128]{4,3,2,1,0:T(2,128)} %bitcast.2, f32[16]{0:T(128)} %low_hbm.1, f32[16]{0:T(128)} %up_hbm.1, f32[32]{0:T(128)} %es_hbm.1, f32[16,128]{1,0:T(8,128)} %bitcast.3), custom_call_target="tpu_custom_call" | custom-call | tf_op jit(solution)/shard_map/pallas_call | solution.py:423
  30.6 1.2 %shard_map.56 = f32[16,2,2,2048]{3,2,1,0:T(2,128)} custom-call(f32[15,2,16,2,128]{4,3,2,1,0:T(2,128)S(1)} %get-tuple-element.9.W, f32[16,2,2,2,128]{4,3,2,1,0:T(2,128)S(1)} %get-tuple-element.10.XR, f32[15,16,2,128]{3,2,1,0:T(2,128)S(1)} %get-tuple-element.11.V, f32[15,16,2,128]{3,2,1,0:T(2,128)S(1)} %get-tuple-element.12.T), custom_call_target="tpu_custom_call" | custom-call | tf_op jit(solution)/shard_map/pallas_call | solution.py:444
